TPU v7x, 256 devices: a whole 4x4x8 slice. The times are simulated.
256 devices in a mesh: group: 4 (over x), dp: 16 (over z_lo, y, core), mp: 4 (over z_hi).
Axes of the slice: x: 4, y: 4, z: 8 (z_hi: 4, z_lo: 2; z = z_hi * 2 + z_lo), core: 2. Of those that a mesh axis runs over, the one named last changes fastest.
Arguments:
- block_input: bfloat16 [768, 8192], P(None, 'dp'), may hold values from -6 to 6
- parent_gate_up: bfloat16 [2, 8192, 14336], P(None, 'dp', ('group', 'mp')), may hold values from -0.0625 to 0.0625
- parent_down: bfloat16 [14336, 8192], P(('group', 'mp'), 'dp'), may hold values from -0.046875 to 0.046875
- variant_gate_up: bfloat16 [4, 2, 8192, 3584], P('group', None, 'dp', 'mp'), may hold values from -0.0625 to 0.0625
- variant_down: bfloat16 [4, 3584, 8192], P('group', 'mp', 'dp'), may hold values from -0.09375 to 0.09375
- widths: int32 [4], P('group'), may hold values from 896 to 3584, as said below
Outputs:
- grad_gate_up: float32 [4, 2, 8192, 3584], P('group', None, 'dp', 'mp')
- grad_down: float32 [4, 3584, 8192], P('group', 'mp', 'dp')
Inputs may be any that keep to these rules, and one draw needn't show every extreme that they name: Variant v uses its hidden units 0 to widths[v] - 1; one variant uses all 3584 of them and another exactly a quarter of 3584.
All inputs are finite; a program needn't handle non-finite values.
Results may differ from a plain program's by a relative error of at most 0.008.
Values may be sent and summed in bfloat16 or wider, within the bound.
No kernel may reach another device: no remote copies, remote signals or barrier semaphores. Data moves between devices by JAX's collectives and lax.ppermute only.
A program may use at most 64 MiB of HBM per device.

v0:
```python
import math
import jax
import jax.numpy as jnp
from jax import lax
from jax.sharding import PartitionSpec as P


def gated_values(pre_act, unit_mask):
    gate_value = pre_act[:, 0].astype(jnp.float32)
    up_value = pre_act[:, 1].astype(jnp.float32)
    sigmoid_gate = jax.nn.sigmoid(gate_value)
    return (gate_value * sigmoid_gate * up_value * unit_mask).astype(jnp.bfloat16)


def pre_gradient(pre_act, unit_mask, hidden_grad):
    gate_value = pre_act[:, 0].astype(jnp.float32)
    up_value = pre_act[:, 1].astype(jnp.float32)
    sigmoid_gate = jax.nn.sigmoid(gate_value)
    masked_grad = hidden_grad * unit_mask
    grad_gate = masked_grad * up_value * sigmoid_gate * (1.0 + gate_value * (1.0 - sigmoid_gate))
    grad_up = masked_grad * gate_value * sigmoid_gate
    return jnp.stack([grad_gate, grad_up], axis=1).astype(jnp.bfloat16)


def body(block_input, parent_gate_up, parent_down, variant_gate_up, variant_down, widths):
    local_gate_up = variant_gate_up[0]
    local_down = variant_down[0]
    local_units = local_down.shape[0]
    all_tokens = block_input.shape[0]
    first_unit = lax.axis_index("mp") * local_units
    unit_index = first_unit + jnp.arange(local_units, dtype=jnp.int32)
    unit_mask = (unit_index < widths[0]).astype(jnp.float32)
    parent_term = jnp.einsum(
        "td,kdf->tkf", block_input, parent_gate_up, preferred_element_type=jnp.float32
    )
    variant_term = jnp.einsum(
        "td,kdf->tkf", block_input, local_gate_up, preferred_element_type=jnp.float32
    )
    parent_rows, variant_rows = (
        lax.psum_scatter(parent_term, "dp", scatter_dimension=0, tiled=True),
        lax.psum_scatter(variant_term, "dp", scatter_dimension=0, tiled=True),
    )
    parent_pre = parent_rows.astype(jnp.bfloat16)
    variant_pre = variant_rows.astype(jnp.bfloat16)
    parent_hidden = gated_values(parent_pre, 1.0)
    parent_all, variant_all = (
        lax.all_gather(parent_hidden, "dp", axis=0, tiled=True),
        lax.all_gather(variant_pre, "dp", axis=0, tiled=True),
    )
    variant_hidden = gated_values(variant_all, unit_mask)
    teacher_part = jnp.dot(parent_all, parent_down, preferred_element_type=jnp.float32)
    student_part = jnp.dot(variant_hidden, local_down, preferred_element_type=jnp.float32)
    teacher = lax.psum(teacher_part, ("group", "mp"))
    student = lax.psum(student_part, "mp")
    loss_scale = 1.0 / math.sqrt(all_tokens)
    output_grad = ((student - teacher) * loss_scale).astype(jnp.bfloat16)
    grad_down = lax.dot_general(
        variant_hidden, output_grad, (((0,), (0,)), ((), ())), preferred_element_type=jnp.float32
    )
    hidden_part = lax.dot_general(
        output_grad, local_down, (((1,), (1,)), ((), ())), preferred_element_type=jnp.float32
    )
    hidden_full = lax.psum(hidden_part, "dp")
    grad_pre = pre_gradient(variant_all, unit_mask, hidden_full)
    grad_gate_up = jnp.einsum(
        "td,tkf->kdf", block_input, grad_pre, preferred_element_type=jnp.float32
    )
    return (grad_gate_up[None], grad_down[None])


def solution(mesh):
    in_specs = (
        P(None, "dp"),
        P(None, "dp", ("group", "mp")),
        P(("group", "mp"), "dp"),
        P("group", None, "dp", "mp"),
        P("group", "mp", "dp"),
        P("group"),
    )
    out_specs = (P("group", None, "dp", "mp"), P("group", "mp", "dp"))
    return jax.shard_map(body, mesh=mesh, in_specs=in_specs, out_specs=out_specs, check_vma=False)
```

profile of v0, /device:TPU:1, one launch (start us, length us, event | category | flops | bytes accessed | tf_op | source)
XLA Modules:
  0.0 652.1 jit_solution(2625803845936884595)
XLA Ops:
  7.2 0.0 copy-start
  7.2 0.0 reduce-scatter.5.cloned.1.call-start
  7.2 1.4 copy-done
  8.7 5.2 fusion.45
  13.9 0.0 copy-start.1
  13.9 0.0 reduce-scatter.5.cloned.1.call-update
  13.9 0.0 reduce-scatter.3.cloned.1.call-start
  13.9 1.1 copy-done.1
  15.0 5.5 fusion.29
  20.5 0.0 reduce-scatter.3.cloned.1.call-update
  20.5 0.0 all-gather.5.cloned.1.call-start
  20.6 66.0 %reduce-scatter.5.cloned.1.call-done = f32[48,2,896]{2,0,1:T(8,128)} async-done(((f32[768,2,896]{2,0,1:T(8,128)}), f32[48,2,896]{2,0,1:T(8,128)}) %reduce-scatter.5.cloned.1.call-update) | async-done | bytes 344080 | tf_op jit(solution)/shard_map/reduce_scatter | solution.py:40
  86.6 1.0 convert_element_type.66
  87.6 0.7 fusion.52
  88.3 0.0 all-gather.5.cloned.1.call-update
  88.3 0.0 all-gather.3.cloned.1.call-start
  88.4 71.3 %reduce-scatter.3.cloned.1.call-done = f32[48,2,896]{2,0,1:T(8,128)} async-done(((f32[768,2,896]{2,0,1:T(8,128)}), f32[48,2,896]{2,0,1:T(8,128)}) %reduce-scatter.3.cloned.1.call-update) | async-done | bytes 344080 | tf_op jit(solution)/shard_map/reduce_scatter | solution.py:41
  159.7 1.7 convert_element_type.60
  161.3 0.0 all-gather.3.cloned.1.call-update
  161.3 0.0 copy-start.2
  161.4 0.0 all-reduce.6.cloned.1.call-start
  161.4 38.0 %all-gather.5.cloned.1.call-done = bf16[768,896]{1,0:T(8,128)(2,1)} async-done(((bf16[48,896]{1,0:T(8,128)(2,1)}), bf16[768,896]{1,0:T(8,128)(2,1)}) %all-gather.5.cloned.1.call-update) | async-done | bytes 1376272 | tf_op jit(solution)/shard_map/all_gather | solution.py:47
  199.4 3.7 fusion.57
  203.1 0.0 all-reduce.6.cloned.1.call-update
  203.1 0.0 all-reduce.4.cloned.1.call-start
  203.8 35.3 %all-gather.3.cloned.1.call-done = bf16[768,2,896]{2,0,1:T(8,128)(2,1)} async-done(((bf16[48,2,896]{2,0,1:T(8,128)(2,1)}), bf16[768,2,896]{2,0,1:T(8,128)(2,1)}) %all-gather.3.cloned.1.call-update) | async-done | bytes 2752528 | tf_op jit(solution)/shard_map/all_gather | solution.py:48
  239.1 0.0 copy-done.2
  239.1 4.0 fusion.31
  243.2 0.0 all-reduce.4.cloned.1.call-update
  243.2 0.0 all-reduce.8.cloned.1.call-start
  243.2 163.2 %all-reduce.6.cloned.1.call-done = f32[768,512]{1,0:T(8,128)} async-done(((f32[768,512]{1,0:T(8,128)}), f32[768,512]{1,0:T(8,128)}) %all-reduce.6.cloned.1.call-update) | async-done | bytes 1572880 | tf_op jit(solution)/shard_map/psum | solution.py:53
  406.4 93.0 %all-reduce.4.cloned.1.call-done = f32[768,512]{1,0:T(8,128)} async-done(((f32[768,512]{1,0:T(8,128)}), f32[768,512]{1,0:T(8,128)}) %all-reduce.4.cloned.1.call-update) | async-done | bytes 1572880 | tf_op jit(solution)/shard_map/psum | solution.py:54
  499.4 2.3 multiply_convert_fusion
  501.7 3.7 fusion.39
  505.4 0.0 all-reduce.8.cloned.1.call-update
  505.5 4.1 convolution_bitcast_fusion
  509.6 123.6 %all-reduce.8.cloned.1.call-done = f32[768,896]{1,0:T(8,128)} async-done(((f32[768,896]{1,0:T(8,128)}), f32[768,896]{1,0:T(8,128)}) %all-reduce.8.cloned.1.call-update) | async-done | bytes 2752528 | tf_op jit(solution)/shard_map/psum | solution.py:63
  633.2 4.0 fusion.36
  637.2 3.5 fusion.26
  640.7 4.6 copy.9
  (1 shorter events, 0.0 us)
Async XLA Ops:
  7.2 1.5 copy-start
  7.2 79.4 %reduce-scatter.5.cloned.1.call-start = ((), (), s32[]{:S(2)}) async-start(), calls=%async_computation.5 | async-start | bytes 5849088 | tf_op jit(solution)/shard_map/reduce_scatter | solution.py:40
  13.9 1.1 copy-start.1
  13.9 145.8 %reduce-scatter.3.cloned.1.call-start = ((), (), s32[]{:S(2)}) async-start(), calls=%async_computation.2 | async-start | bytes 5849088 | tf_op jit(solution)/shard_map/reduce_scatter | solution.py:41
  20.5 178.9 %all-gather.5.cloned.1.call-start = ((), (), s32[]{:S(2)}) async-start(), calls=%async_computation.6 | async-start | bytes 1462272 | tf_op jit(solution)/shard_map/all_gather | solution.py:47
  88.3 150.8 %all-gather.3.cloned.1.call-start = ((), (), s32[]{:S(2)}) async-start(), calls=%async_computation.3 | async-start | bytes 2924544 | tf_op jit(solution)/shard_map/all_gather | solution.py:48
  161.3 77.8 %copy-start.2 = (bf16[1,896,512]{2,1,0:T(8,128)(2,1)S(1)}, bf16[1,896,512]{2,1,0:T(8,128)(2,1)}, u32[]{:S(2)}) copy-start(bf16[1,896,512]{2,1,0:T(8,128)(2,1)} %param.10) | copy-start | bytes 2752516
  161.4 245.1 %all-reduce.6.cloned.1.call-start = ((), (), s32[]{:S(2)}) async-start(), calls=%async_computation.7 | async-start | bytes 3145728 | tf_op jit(solution)/shard_map/psum | solution.py:53
  203.1 296.3 %all-reduce.4.cloned.1.call-start = ((), (), s32[]{:S(2)}) async-start(), calls=%async_computation.4 | async-start | bytes 3145728 | tf_op jit(solution)/shard_map/psum | solution.py:54
  243.2 390.0 %all-reduce.8.cloned.1.call-start = ((), (), s32[]{:S(2)}) async-start(), calls=%async_computation.8 | async-start | bytes 5505024 | tf_op jit(solution)/shard_map/psum | solution.py:63
Sparse Core Ops, SparseCore 0:
  14.0 72.5 reduce-scatter.4
  89.1 70.4 reduce-scatter.2
  162.1 37.2 all-gather.4
  201.6 37.4 all-gather.2
  242.2 164.1 all-reduce.5
  409.5 89.8 all-reduce.3
  505.6 127.5 all-reduce.7
where the time goes:
time: 653 us; the launch traced here: 652 us
  waiting for transfers between devices  590 us (90%)
  matrix products  29.8 us (5%)
  between operations  14.8 us (2%)
  other arithmetic  9.67 us (1%)
  local copies, waits for them, and re-layouts  7.1 us (1%)
    psum x1, waiting for transfers between devices, body(): teacher = lax.psum(teacher_part, ('group', 'mp'))  163 us
    psum x1, waiting for transfers between devices, body(): hidden_full = lax.psum(hidden_part, 'dp')  124 us
    psum x1, waiting for transfers between devices, body(): student = lax.psum(student_part, 'mp')  93 us
    reduce_scatter x1, waiting for transfers between devices, body(): lax.psum_scatter(variant_term, 'dp', scatter_dimension=0, tiled=True)  71.3 us
    reduce_scatter x1, waiting for transfers between devices, body(): lax.psum_scatter(parent_term, 'dp', scatter_dimension=0, tiled=True)  66 us
    all_gather x1, waiting for transfers between devices, body(): lax.all_gather(parent_hidden, 'dp', axis=0, tiled=True)  38 us
    all_gather x1, waiting for transfers between devices, body(): lax.all_gather(variant_pre, 'dp', axis=0, tiled=True)  35.3 us
  transfers between devices with their start and end apart: 7, of which 7 were waited for; matrix products, arithmetic and copies ran while one was open for 3% of the time, Pallas kernels for 0%

commit v1 on v0

--- a/solution.py
+++ b/solution.py
@@ -44,7 +44,9 @@
     variant_pre = variant_rows.astype(jnp.bfloat16)
     parent_hidden = gated_values(parent_pre, 1.0)
     parent_all, variant_all = (
-        lax.all_gather(parent_hidden, "dp", axis=0, tiled=True),
+        jnp.concatenate(
+            lax.all_to_all(jnp.stack([parent_hidden] * lax.axis_size("dp")), "dp", 0, 0), axis=0
+        ),
         lax.all_gather(variant_pre, "dp", axis=0, tiled=True),
     )
     variant_hidden = gated_values(variant_all, unit_mask)

time: 653 us -> 620 us (0.949)
  waiting for transfers between devices: 590 us -> 530 us
  blocking collectives: 0 us -> 29.1 us
    all_gather x1 -> x0, waiting for transfers between devices: 38 us -> none  [body(): lax.all_gather(parent_hidden, 'dp', axis=0, tiled=True)]
    all_to_all x0 -> x1, blocking collectives: none -> 29.1 us  [body(): lax.all_to_all(jnp.stack([parent_hidden] * lax.axis_size('dp')), 'dp', 0, 0)]
    all_gather x1, waiting for transfers between devices: 35.3 us -> 13.1 us  [body(): lax.all_gather(variant_pre, 'dp', axis=0, tiled=True)]
  transfers between devices with their start and end apart: 7 -> 6, of which waited for: 7 -> 6; matrix products, arithmetic and copies ran while one was open for 3% -> 3% of each run, Pallas kernels for 0% -> 0%
where the time goes in v1:
time: 620 us; the launch traced here: 619 us
  waiting for transfers between devices  530 us (85%)
  matrix products  29.4 us (5%)
  blocking collectives  29.1 us (5%)
  between operations  14.8 us (2%)
  other arithmetic  9.03 us (1%)
  local copies, waits for them, and re-layouts  7.2 us (1%)
    psum x1, waiting for transfers between devices, body(): teacher = lax.psum(teacher_part, ('group', 'mp'))  163 us
    psum x1, waiting for transfers between devices, body(): hidden_full = lax.psum(hidden_part, 'dp')  124 us
    psum x1, waiting for transfers between devices, body(): student = lax.psum(student_part, 'mp')  93 us
    reduce_scatter x1, waiting for transfers between devices, body(): lax.psum_scatter(parent_term, 'dp', scatter_dimension=0, tiled=True)  71.3 us
    reduce_scatter x1, waiting for transfers between devices, body(): lax.psum_scatter(variant_term, 'dp', scatter_dimension=0, tiled=True)  66 us
    all_to_all x1, blocking collectives, body(): lax.all_to_all(jnp.stack([parent_hidden] * lax.axis_size('dp')), 'dp', 0, 0)  29.1 us
    all_gather x1, waiting for transfers between devices, body(): lax.all_gather(variant_pre, 'dp', axis=0, tiled=True)  13.1 us
  transfers between devices with their start and end apart: 6, of which 6 were waited for; matrix products, arithmetic and copies ran while one was open for 3% of the time, Pallas kernels for 0%

profile of v1, /device:TPU:1, one launch (start us, length us, event | category | flops | bytes accessed | tf_op | source)
XLA Modules:
  0.0 619.5 jit_solution(10581348596636356272)
XLA Ops:
  7.2 0.0 copy-start
  7.2 0.0 reduce-scatter.3.cloned.1.call-start
  7.2 1.4 copy-done
  8.7 5.2 fusion.29
  13.9 0.0 copy-start.1
  13.9 0.0 reduce-scatter.3.cloned.1.call-update
  13.9 0.0 reduce-scatter.5.cloned.1.call-start
  13.9 1.1 copy-done.1
  15.0 5.5 fusion.45
  20.5 0.0 reduce-scatter.5.cloned.1.call-update
  20.5 0.0 all-gather.2.cloned.1.call-start
  20.6 66.0 %reduce-scatter.3.cloned.1.call-done = f32[48,2,896]{2,0,1:T(8,128)} async-done(((f32[768,2,896]{2,0,1:T(8,128)}), f32[48,2,896]{2,0,1:T(8,128)}) %reduce-scatter.3.cloned.1.call-update) | async-done | bytes 344080 | tf_op jit(solution)/shard_map/reduce_scatter | solution.py:41
  86.6 1.7 convert_element_type.66
  88.2 0.0 all-gather.2.cloned.1.call-update
  88.3 0.0 all-reduce.6.cloned.1.call-start
  88.3 71.3 %reduce-scatter.5.cloned.1.call-done = f32[48,2,896]{2,0,1:T(8,128)} async-done(((f32[768,2,896]{2,0,1:T(8,128)}), f32[48,2,896]{2,0,1:T(8,128)}) %reduce-scatter.5.cloned.1.call-update) | async-done | bytes 344080 | tf_op jit(solution)/shard_map/reduce_scatter | solution.py:40
  159.6 1.0 convert_element_type.72
  160.7 0.1 fusion.52
  160.7 0.1 stack.11
  160.8 29.1 %all_to_all.5 = bf16[16,48,896]{2,1,0:T(8,128)(2,1)S(1)} all-to-all(bf16[16,48,896]{2,1,0:T(8,128)(2,1)S(1)} %stack.11), channel_id=1, replica_groups=mesh['group'=4,'dp'=16,'mp'=4] {'dp'}, dimensions={0} | all-to-all | bytes 2752512 | tf_op jit(solution)/shard_map/all_to_all | solution.py:48
  189.9 0.0 copy-start.2
  190.0 3.4 fusion.57
  193.3 0.0 all-reduce.6.cloned.1.call-update
  193.4 0.0 all-reduce.4.cloned.1.call-start
  194.1 13.1 %all-gather.2.cloned.1.call-done = bf16[768,2,896]{2,0,1:T(8,128)(2,1)} async-done(((bf16[48,2,896]{2,0,1:T(8,128)(2,1)}), bf16[768,2,896]{2,0,1:T(8,128)(2,1)}) %all-gather.2.cloned.1.call-update) | async-done | bytes 2752528 | tf_op jit(solution)/shard_map/all_gather | solution.py:50
  207.2 0.0 copy-done.2
  207.2 4.0 fusion.31
  211.2 0.0 all-reduce.4.cloned.1.call-update
  211.2 0.0 all-reduce.8.cloned.1.call-start
  211.3 162.5 %all-reduce.6.cloned.1.call-done = f32[768,512]{1,0:T(8,128)} async-done(((f32[768,512]{1,0:T(8,128)}), f32[768,512]{1,0:T(8,128)}) %all-reduce.6.cloned.1.call-update) | async-done | bytes 1572880 | tf_op jit(solution)/shard_map/psum | solution.py:55
  373.8 93.0 %all-reduce.4.cloned.1.call-done = f32[768,512]{1,0:T(8,128)} async-done(((f32[768,512]{1,0:T(8,128)}), f32[768,512]{1,0:T(8,128)}) %all-reduce.4.cloned.1.call-update) | async-done | bytes 1572880 | tf_op jit(solution)/shard_map/psum | solution.py:56
  466.8 2.3 multiply_convert_fusion
  469.1 3.7 fusion.39
  472.8 0.0 all-reduce.8.cloned.1.call-update
  472.9 4.1 convolution_bitcast_fusion
  477.0 123.6 %all-reduce.8.cloned.1.call-done = f32[768,896]{1,0:T(8,128)} async-done(((f32[768,896]{1,0:T(8,128)}), f32[768,896]{1,0:T(8,128)}) %all-reduce.8.cloned.1.call-update) | async-done | bytes 2752528 | tf_op jit(solution)/shard_map/psum | solution.py:65
  600.6 4.0 fusion.36
  604.6 3.4 fusion.26
  608.1 4.6 copy.9
  (1 shorter events, 0.0 us)
Async XLA Ops:
  7.2 1.5 copy-start
  7.2 79.4 %reduce-scatter.3.cloned.1.call-start = ((), (), s32[]{:S(2)}) async-start(), calls=%async_computation.3 | async-start | bytes 5849088 | tf_op jit(solution)/shard_map/reduce_scatter | solution.py:41
  13.9 1.1 copy-start.1
  13.9 145.8 %reduce-scatter.5.cloned.1.call-start = ((), (), s32[]{:S(2)}) async-start(), calls=%async_computation.6 | async-start | bytes 5849088 | tf_op jit(solution)/shard_map/reduce_scatter | solution.py:40
  20.5 186.7 %all-gather.2.cloned.1.call-start = ((), (), s32[]{:S(2)}) async-start(), calls=%async_computation.4 | async-start | bytes 2924544 | tf_op jit(solution)/shard_map/all_gather | solution.py:50
  88.3 285.6 %all-reduce.6.cloned.1.call-start = ((), (), s32[]{:S(2)}) async-start(), calls=%async_computation.7 | async-start | bytes 3145728 | tf_op jit(solution)/shard_map/psum | solution.py:55
  189.9 17.3 %copy-start.2 = (bf16[1,896,512]{2,1,0:T(8,128)(2,1)S(1)}, bf16[1,896,512]{2,1,0:T(8,128)(2,1)}, u32[]{:S(2)}) copy-start(bf16[1,896,512]{2,1,0:T(8,128)(2,1)} %param.10) | copy-start | bytes 2752516
  193.4 273.5 %all-reduce.4.cloned.1.call-start = ((), (), s32[]{:S(2)}) async-start(), calls=%async_computation.5 | async-start | bytes 3145728 | tf_op jit(solution)/shard_map/psum | solution.py:56
  211.2 389.4 %all-reduce.8.cloned.1.call-start = ((), (), s32[]{:S(2)}) async-start(), calls=%async_computation.8 | async-start | bytes 5505024 | tf_op jit(solution)/shard_map/psum | solution.py:65
Sparse Core Ops, SparseCore 0:
  14.0 72.5 reduce-scatter.2
  89.1 70.4 reduce-scatter.4
  162.0 45.1 all-gather.1
  210.3 163.5 all-reduce.5
  376.9 89.8 all-reduce.3
  473.0 127.5 all-reduce.7
